TPU v7x, 32 devices: a whole 2x2x4 slice. The times are simulated.
32 devices in a mesh: row: 4 (over x, core), col: 8 (over z, y).
Axes of the slice: x: 2, y: 2, z: 4, core: 2. Of those that a mesh axis runs over, the one named last changes fastest.
Arguments:
- weight: bfloat16 [16384, 16384], P('row', 'col'), may hold values from -0.046875 to 0.046875
- momentum: float32 [16384, 16384], P('row', 'col'), may hold values from -36 to 36
- right_factor: float32 [16384, 512], P(('col', 'row')), may hold values from -0.046875 to 0.046875
- output_grads: bfloat16 [1024, 16384], P('col', 'row'), may hold values from -0.1875 to 0.1875
- activations: bfloat16 [1024, 16384], P('row', 'col'), may hold values from -6 to 6
Outputs:
- new_weight: bfloat16 [16384, 16384], P('row', 'col')
- new_momentum: float32 [16384, 16384], P('row', 'col')
- new_factor: float32 [16384, 512], P(('col', 'row'))
All inputs are finite; a program needn't handle non-finite values.
Results may differ from a plain program's by a relative error of at most 0.0004.
Values may be sent and summed in bfloat16 or wider, within the bound.
No kernel may reach another device: no remote copies, remote signals or barrier semaphores. Data moves between devices by JAX's collectives and lax.ppermute only.
A program may use at most 192 MiB of HBM per device.

v0:
```python
import math
import jax
import jax.numpy as jnp
from jax import lax
from jax.sharding import PartitionSpec as P

D_OUT = 16384
D_IN = 16384
FULL_PRECISION = lax.Precision.HIGHEST
MOMENTUM_DECAY = 0.95
LEARN_RATE = 0.002
NORM_EPS = 1e-06


def contract_rows(first, second):
    return lax.dot_general(
        first,
        second,
        (((0,), (0,)), ((), ())),
        precision=FULL_PRECISION,
        preferred_element_type=jnp.float32,
    )


def outer_rows(first, second):
    return lax.dot_general(
        first,
        second,
        (((1,), (1,)), ((), ())),
        precision=FULL_PRECISION,
        preferred_element_type=jnp.float32,
    )


def orthogonalize(left_factor, gram_matrix):
    lower_factor = jnp.linalg.cholesky(gram_matrix)
    identity = jnp.eye(gram_matrix.shape[0], dtype=gram_matrix.dtype)
    inverse = jax.scipy.linalg.solve_triangular(lower_factor, identity, lower=True)
    return outer_rows(left_factor, inverse)


def body(weight, momentum, right_factor, output_grads, activations):
    grads_whole = lax.all_gather(output_grads, "col", axis=0, tiled=True)
    grad_tile = lax.dot_general(
        grads_whole,
        lax.all_gather(activations, "row", axis=0, tiled=True),
        (((0,), (0,)), ((), ())),
        preferred_element_type=jnp.float32,
    )
    buffer = momentum + grad_tile
    factor_block = lax.all_gather(right_factor, "row", axis=0, tiled=True)
    left_partial = jnp.dot(
        buffer, factor_block, precision=FULL_PRECISION, preferred_element_type=jnp.float32
    )
    left_factor = lax.psum(left_partial, "col")
    gram_matrix = lax.psum(contract_rows(left_factor, left_factor), "row")
    ortho_left = orthogonalize(left_factor, gram_matrix)
    right_piece = lax.psum_scatter(
        contract_rows(buffer, ortho_left), "row", scatter_dimension=0, tiled=True
    )
    column_squares = lax.psum(jnp.sum(right_piece * right_piece, axis=0), ("row", "col"))
    column_norm = jnp.sqrt(column_squares + NORM_EPS)
    new_factor = right_piece / column_norm
    projected = lax.all_gather(right_piece, "row", axis=0, tiled=True)
    new_momentum = buffer - (1.0 - MOMENTUM_DECAY) * outer_rows(ortho_left, projected)
    factor_cols = projected / column_norm
    step_scale = LEARN_RATE * math.sqrt(max(D_OUT, D_IN))
    new_weight = (
        weight.astype(jnp.float32) - step_scale * outer_rows(ortho_left, factor_cols)
    ).astype(jnp.bfloat16)
    return (new_weight, new_momentum, new_factor)


def solution(mesh):
    in_specs = (
        P("row", "col"),
        P("row", "col"),
        P(("col", "row"), None),
        P("col", "row"),
        P("row", "col"),
    )
    out_specs = (P("row", "col"), P("row", "col"), P(("col", "row"), None))
    return jax.shard_map(body, mesh=mesh, in_specs=in_specs, out_specs=out_specs, check_vma=False)
```

profile of v0, /device:TPU:0, one launch (start us, length us, event | category | flops | bytes accessed | tf_op | source)
XLA Modules:
  0.0 1043.1 jit_solution(17681060143477142184)
XLA Ops:
  7.2 0.7 all-gather.7.cloned.1.call-update
  7.9 0.7 all-gather.5.cloned.1.call-update
  8.7 0.7 all-gather.9.cloned.1.call-update
  9.4 37.3 %all-gather.7.cloned.1.call-done = bf16[1024,2048]{1,0:T(8,128)(2,1)} async-done(((bf16[256,2048]{1,0:T(8,128)(2,1)}), bf16[1024,2048]{1,0:T(8,128)(2,1)}) %all-gather.7.cloned.1.call-update) | async-done | bytes 4194320 | tf_op jit(solution)/shard_map/all_gather | solution.py:46
  46.7 126.6 %all-gather.5.cloned.1.call-done = bf16[1024,4096]{1,0:T(8,128)(2,1)} async-done(((bf16[128,4096]{1,0:T(8,128)(2,1)}), bf16[1024,4096]{1,0:T(8,128)(2,1)}) %all-gather.5.cloned.1.call-update) | async-done | bytes 8388624 | tf_op jit(solution)/shard_map/all_gather | solution.py:43
  173.4 36.2 %convolution_add_fusion = f32[4096,2048]{1,0:T(8,128)} fusion(f32[4096,2048]{1,0:T(8,128)} %param.6, bf16[1024,4096]{1,0:T(8,128)(2,1)} %all-gather.5.cloned.1.call-done, bf16[1024,2048]{1,0:T(8,128)(2,1)} %all-gather.7.cloned.1.call-done), kind=kOutput, calls=%fused_computation.4 | convolution fusion | flops 17188257792 | bytes 79691776 | tf_op jit(solution)/shard_map/dot_general | solution.py:44
  209.6 65.1 %fusion.43 = f32[4096,512]{1,0:T(8,128)} fusion(f32[4096,2048]{1,0:T(8,128)} %convolution_add_fusion, f32[2048,512]{1,0:T(8,128)} %all-gather.9.cloned.1.call-done), kind=kOutput, calls=%fused_computation.85 | convolution fusion | flops 51539607552 | bytes 46137344 | tf_op jit(solution)/shard_map/dot_general | solution.py:52
  275.0 267.8 %all-reduce.4.cloned.1.call-done = f32[4096,512]{1,0:T(8,128)} async-done(((f32[4096,512]{1,0:T(8,128)}), f32[4096,512]{1,0:T(8,128)}) %all-reduce.4.cloned.1.call-update) | async-done | bytes 8388624 | tf_op jit(solution)/shard_map/psum | solution.py:55
  542.8 18.5 %fusion.44 = f32[512,512]{0,1:T(8,128)} fusion(f32[4096,512]{1,0:T(8,128)} %all-reduce.4.cloned.1.call-done), kind=kOutput, calls=%fused_computation.86 | convolution fusion | flops 12884901888 | bytes 9437184 | tf_op jit(solution)/shard_map/dot_general | solution.py:16
  561.4 0.8 iota_compare_fusion
  562.3 34.6 %all-reduce.6.cloned.1.call-done = f32[512,512]{0,1:T(8,128)} async-done(((f32[512,512]{0,1:T(8,128)}), f32[512,512]{0,1:T(8,128)}) %all-reduce.6.cloned.1.call-update) | async-done | bytes 1048592 | tf_op jit(solution)/shard_map/psum | solution.py:56
  596.9 1.6 copy.9
  598.4 1.4 fusion.10
  599.9 11.7 %cholesky.104 = f32[128,128]{1,0:T(8,128)S(1)} custom-call(f32[128,128]{1,0:T(8,128)S(1)} %cholesky.266), custom_call_target="Cholesky" | custom-call | tf_op jit(solution)/shard_map/jit(cholesky)/cholesky | solution.py:36
  611.7 9.8 custom-call.31
  622.3 11.7 %cholesky.217 = f32[128,128]{1,0:T(8,128)S(1)} custom-call(f32[128,128]{1,0:T(8,128)S(1)} %cholesky.270), custom_call_target="Cholesky" | custom-call | tf_op jit(solution)/shard_map/jit(cholesky)/cholesky | solution.py:36
  634.0 18.5 %custom-call.32 = f32[1,128,128]{1,2,0:T(8,128)S(1)} custom-call(f32[1,128,128]{2,1,0:T(8,128)S(1)} %get-tuple-element.27), custom_call_target="InvertDiagBlocksLowerTriangular" | custom-call | tf_op jit(solution)/shard_map/jit(cholesky)/cholesky | solution.py:36
  653.2 11.7 %cholesky.238 = f32[128,128]{1,0:T(8,128)S(1)} custom-call(f32[128,128]{1,0:T(8,128)S(1)} %cholesky.275), custom_call_target="Cholesky" | custom-call | tf_op jit(solution)/shard_map/jit(cholesky)/cholesky | solution.py:36
  665.0 0.6 compare_reduce_fusion.1
  665.6 9.8 custom-call.33
  676.0 11.7 %cholesky.255 = f32[128,128]{1,0:T(8,128)S(1)} custom-call(f32[128,128]{1,0:T(8,128)S(1)} %convolution_subtract_fusion.5), custom_call_target="Cholesky" | custom-call | tf_op jit(solution)/shard_map/jit(cholesky)/cholesky | solution.py:36
  687.7 0.7 compare_reduce_fusion
  688.4 1.0 compare_reduce_fusion.2
  692.0 10.1 while.1
  692.1 0.5 fusion.67
  692.6 1.9 bitcast_dynamic-update-slice_fusion.2
  694.6 0.5 fusion.67
  695.1 1.9 bitcast_dynamic-update-slice_fusion.2
  697.1 0.5 fusion.67
  697.6 1.9 bitcast_dynamic-update-slice_fusion.2
  699.6 0.5 fusion.67
  700.2 1.9 bitcast_dynamic-update-slice_fusion.2
  702.1 40.1 %custom-call.34 = f32[4,128,128]{1,2,0:T(8,128)S(1)} custom-call(f32[4,128,128]{2,1,0:T(8,128)} %get-tuple-element.10), custom_call_target="InvertDiagBlocksLowerTriangular" | custom-call | tf_op jit(solution)/shard_map/jit(_solve_triangular)/triangular_solve | solution.py:38
  742.2 1.1 fusion.21
  743.7 0.4 fusion.33
  744.1 0.4 convolution_subtract_fusion
  744.5 0.4 fusion.31
  745.0 0.6 convolution_subtract_fusion.2
  745.6 0.4 fusion.30
  746.0 17.1 %fusion.2 = f32[4096,512]{1,0:T(8,128)S(1)} fusion(f32[4096,512]{1,0:T(8,128)} %all-reduce.4.cloned.1.call-done, f32[128,512]{1,0:T(8,128)S(1)} %fusion.30, f32[128,512]{1,0:T(8,128)S(1)} %fusion.31, f32[128,512]{1,0:T(8,128)S(1)} %fusion.33, f32[128,512]{1,0:T(8,128)S(1)} %fusion.21), kind=kOutput, calls=%fused_computation.16 | convolution fusion | flops 12885688320 | bytes 17825792 | tf_op jit(solution)/shard_map/dot_general | solution.py:26
  763.2 3.2 copy-done
  766.4 58.7 %fusion.45 = f32[2048,512]{1,0:T(8,128)} fusion(f32[4096,2048]{1,0:T(8,128)} %convolution_add_fusion, f32[4096,512]{1,0:T(8,128)S(1)} %fusion.2), kind=kOutput, calls=%fused_computation.87 | convolution fusion | flops 51539607552 | bytes 46137344 | tf_op jit(solution)/shard_map/dot_general | solution.py:16
  825.2 45.2 %reduce-scatter.2.cloned.1.call-done = f32[512,512]{1,0:T(8,128)} async-done(((f32[2048,512]{1,0:T(8,128)}), f32[512,512]{1,0:T(8,128)}) %reduce-scatter.2.cloned.1.call-update) | async-done | bytes 1048592 | tf_op jit(solution)/shard_map/reduce_scatter | solution.py:58
  870.4 1.3 multiply_reduce_fusion
  871.7 39.7 %psum.23 = f32[512]{0:T(512)S(1)} all-reduce(f32[512]{0:T(512)S(1)} %multiply_reduce_fusion), channel_id=1, replica_groups=mesh['row'=4,'col'=8] {'row','col'}, use_global_device_ids=true, to_apply=%region_12.13 | all-reduce | flops 512 | bytes 4096 | tf_op jit(solution)/shard_map/psum | solution.py:61
  911.4 2.3 broadcast_divide_fusion
  913.8 62.5 %multiply_subtract_fusion = f32[4096,2048]{1,0:T(8,128)} fusion(f32[4096,2048]{1,0:T(8,128)} %convolution_add_fusion, f32[4096,512]{1,0:T(8,128)} %copy-done, f32[2048,512]{1,0:T(8,128)} %all-gather.11.cloned.1.call-done), kind=kOutput, calls=%fused_computation.2 | convolution fusion | flops 51556384768 | bytes 79691776 | tf_op jit(solution)/shard_map/dot_general | solution.py:26
  976.3 59.6 %subtract_convert_fusion = bf16[4096,2048]{1,0:T(8,128)(2,1)} fusion(bf16[4096,2048]{1,0:T(8,128)(2,1)} %param.5, f32[4096,512]{1,0:T(8,128)} %copy-done, f32[2048,512]{1,0:T(8,128)S(1)} %copy-done.1, f32[512]{0:T(512)S(1)} %add_sqrt_fusion), kind=kOutput, calls=%fused_computation.3 | convolution fusion | flops 51574210560 | bytes 46139392 | tf_op jit(solution)/shard_map/dot_general | solution.py:26
  (41 shorter events, 3.7 us)
Async XLA Ops:
  7.2 39.6 %all-gather.7.cloned.1.call-start = ((), (), s32[]{:S(2)}) async-start(), calls=%async_computation.2 | async-start | bytes 5242880 | tf_op jit(solution)/shard_map/all_gather | solution.py:46
  7.9 165.5 %all-gather.5.cloned.1.call-start = ((), (), s32[]{:S(2)}) async-start(), calls=%async_computation.1 | async-start | bytes 9437184 | tf_op jit(solution)/shard_map/all_gather | solution.py:43
  8.6 201.0 %all-gather.9.cloned.1.call-start = ((), (), s32[]{:S(2)}) async-start(), calls=%async_computation.3 | async-start | bytes 5242880 | tf_op jit(solution)/shard_map/all_gather | solution.py:51
  9.4 533.4 %all-reduce.4.cloned.1.call-start = ((), (), s32[]{:S(2)}) async-start(), calls=%async_computation.4 | async-start | bytes 16777216 | tf_op jit(solution)/shard_map/psum | solution.py:55
  274.7 322.2 %all-reduce.6.cloned.1.call-start = ((), (), s32[]{:S(2)}) async-start(), calls=%async_computation.5 | async-start | bytes 2097152 | tf_op jit(solution)/shard_map/psum | solution.py:56
  561.3 309.0 %reduce-scatter.2.cloned.1.call-start = ((), (), s32[]{:S(2)}) async-start(), calls=%async_computation.6 | async-start | bytes 5242880 | tf_op jit(solution)/shard_map/reduce_scatter | solution.py:58
  763.2 3.2 copy-start
  825.1 88.6 %all-gather.11.cloned.1.call-start = ((), (), s32[]{:S(2)}) async-start(), calls=%async_computation.7 | async-start | bytes 5242880 | tf_op jit(solution)/shard_map/all_gather | solution.py:64
  913.8 62.5 %copy-start.1 = (f32[2048,512]{1,0:T(8,128)S(1)}, f32[2048,512]{1,0:T(8,128)}, u32[]{:S(2)}) copy-start(f32[2048,512]{1,0:T(8,128)} %all-gather.11.cloned.1.call-done) | copy-start | bytes 12582916
Sparse Core Ops, SparseCore 0:
  9.5 37.1 all-gather.6
  48.9 124.4 all-gather.4
  174.9 32.6 all-gather.8
  274.8 267.9 all-reduce.3
  561.5 35.3 all-reduce.5
  825.3 45.0 reduce-scatter.1
  871.9 34.7 all-gather.10
where the time goes:
time: 1050 us; the launch traced here: 1040 us
  waiting for transfers between devices  514 us (49%)
  matrix products  323 us (31%)
  other arithmetic  134 us (13%)
  blocking collectives  39.7 us (4%)
  between operations  17.2 us (2%)
  local copies, waits for them, and re-layouts  15 us (1%)
    psum x1, waiting for transfers between devices, body(): left_factor = lax.psum(left_partial, 'col')  268 us
    dot_general x3, matrix products, outer_rows(): lax.dot_general(first, second, (((1,), (1,)), ((), ())), precision=FULL_P...  139 us
    all_gather x1, waiting for transfers between devices, body(): grads_whole = lax.all_gather(output_grads, 'col', axis=0, tiled=True)  127 us
    another operation x14, other arithmetic, orthogonalize(): lower_factor = jnp.linalg.cholesky(gram_matrix)  87.4 us
    dot_general x2, matrix products, contract_rows(): lax.dot_general(first, second, (((0,), (0,)), ((), ())), precision=FULL_P...  77.2 us
    dot_general x1, matrix products, body(): jnp.dot(buffer, factor_block, precision=FULL_PRECISION, preferred_element...  65.1 us
    reduce_scatter x1, waiting for transfers between devices, body(): lax.psum_scatter(contract_rows(buffer, ortho_left), 'row', scatter_dimens...  45.2 us
    another operation x3, other arithmetic, orthogonalize(): jax.scipy.linalg.solve_triangular(lower_factor, identity, lower=True)  40.3 us
  transfers between devices with their start and end apart: 7, of which 5 were waited for; matrix products, arithmetic and copies ran while one was open for 4% of the time, Pallas kernels for 0%

commit v1 on v0

--- a/solution.py
+++ b/solution.py
@@ -52,7 +52,8 @@
     left_partial = jnp.dot(
         buffer, factor_block, precision=FULL_PRECISION, preferred_element_type=jnp.float32
     )
-    left_factor = lax.psum(left_partial, "col")
+    parts = lax.all_gather(left_partial, "col")
+    left_factor = jnp.sum(parts, axis=0)
     gram_matrix = lax.psum(contract_rows(left_factor, left_factor), "row")
     ortho_left = orthogonalize(left_factor, gram_matrix)
     right_piece = lax.psum_scatter(

time: 1050 us -> 2070 us (1.97)
  waiting for transfers between devices: 514 us -> 1510 us
  other arithmetic: 134 us -> 159 us
    all_gather x0 -> x1, waiting for transfers between devices: none -> 1260 us  [body(): parts = lax.all_gather(left_partial, 'col')]
    psum x1 -> x0, waiting for transfers between devices: 268 us -> none  [body(): left_factor = lax.psum(left_partial, 'col')]
    reduce_sum x0 -> x1, other arithmetic: none -> 24.8 us  [body(): left_factor = jnp.sum(parts, axis=0)]
  transfers between devices with their start and end apart: 7 -> 7, of which waited for: 5 -> 5; matrix products, arithmetic and copies ran while one was open for 4% -> 2% of each run, Pallas kernels for 0% -> 0%
where the time goes in v1:
time: 2070 us
  waiting for transfers between devices  1510 us (73%)
  matrix products  323 us (16%)
  other arithmetic  159 us (8%)
  blocking collectives  39.7 us (2%)
    all_gather x1, waiting for transfers between devices, body(): parts = lax.all_gather(left_partial, 'col')  1260 us
    dot_general x3, matrix products, outer_rows(): lax.dot_general(first, second, (((1,), (1,)), ((), ())), precision=FULL_P...  139 us
    all_gather x1, waiting for transfers between devices, body(): grads_whole = lax.all_gather(output_grads, 'col', axis=0, tiled=True)  127 us
    another operation x14, other arithmetic, orthogonalize(): lower_factor = jnp.linalg.cholesky(gram_matrix)  87.5 us
    dot_general x2, matrix products, contract_rows(): lax.dot_general(first, second, (((0,), (0,)), ((), ())), precision=FULL_P...  77.1 us
    dot_general x1, matrix products, body(): jnp.dot(buffer, factor_block, precision=FULL_PRECISION, preferred_element...  65.1 us
    reduce_scatter x1, waiting for transfers between devices, body(): lax.psum_scatter(contract_rows(buffer, ortho_left), 'row', scatter_dimens...  45.2 us
  transfers between devices with their start and end apart: 7, of which 5 were waited for; matrix products, arithmetic and copies ran while one was open for 2% of the time, Pallas kernels for 0%

profile of v1, /device:TPU:0, one launch (start us, length us, event | category | flops | bytes accessed | tf_op | source)
XLA Modules:
  0.0 2066.6 jit_solution(5031325351384720841)
XLA Ops:
  7.2 0.7 all-gather.9.cloned.1.call-update
  7.9 0.7 all-gather.7.cloned.1.call-update
  8.7 0.7 all-gather.11.cloned.1.call-update
  9.4 37.3 %all-gather.9.cloned.1.call-done = bf16[1024,2048]{1,0:T(8,128)(2,1)} async-done(((bf16[256,2048]{1,0:T(8,128)(2,1)}), bf16[1024,2048]{1,0:T(8,128)(2,1)}) %all-gather.9.cloned.1.call-update) | async-done | bytes 4194320 | tf_op jit(solution)/shard_map/all_gather | solution.py:46
  46.7 126.6 %all-gather.7.cloned.1.call-done = bf16[1024,4096]{1,0:T(8,128)(2,1)} async-done(((bf16[128,4096]{1,0:T(8,128)(2,1)}), bf16[1024,4096]{1,0:T(8,128)(2,1)}) %all-gather.7.cloned.1.call-update) | async-done | bytes 8388624 | tf_op jit(solution)/shard_map/all_gather | solution.py:43
  173.4 36.2 %convolution_add_fusion = f32[4096,2048]{1,0:T(8,128)} fusion(f32[4096,2048]{1,0:T(8,128)} %param.6, bf16[1024,4096]{1,0:T(8,128)(2,1)} %all-gather.7.cloned.1.call-done, bf16[1024,2048]{1,0:T(8,128)(2,1)} %all-gather.9.cloned.1.call-done), kind=kOutput, calls=%fused_computation.4 | convolution fusion | flops 17188257792 | bytes 79691776 | tf_op jit(solution)/shard_map/dot_general | solution.py:44
  209.6 65.1 %fusion.43 = f32[4096,512]{1,0:T(8,128)} fusion(f32[4096,2048]{1,0:T(8,128)} %convolution_add_fusion, f32[2048,512]{1,0:T(8,128)} %all-gather.11.cloned.1.call-done), kind=kOutput, calls=%fused_computation.85 | convolution fusion | flops 51539607552 | bytes 46137344 | tf_op jit(solution)/shard_map/dot_general | solution.py:52
  275.0 1264.7 %all-gather.15.cloned.1.call-done = f32[32768,512]{1,0:T(8,128)} async-done(((f32[4096,512]{1,0:T(8,128)}), f32[32768,512]{1,0:T(8,128)}) %all-gather.15.cloned.1.call-update) | async-done | bytes 67108880 | tf_op jit(solution)/shard_map/all_gather | solution.py:55
  1539.7 24.8 %reduce_sum.18 = f32[4096,512]{1,0:T(8,128)} reduce(f32[8,4096,512]{2,1,0:T(8,128)} %bitcast, f32[]{:T(128)} %constant.142.clone.1), dimensions={0}, to_apply=%region_0.0 | reduce | flops 14680064 | bytes 75497472 | tf_op jit(solution)/shard_map/reduce_sum | solution.py:56
  1564.5 18.4 fusion.44
  1583.0 0.8 iota_compare_fusion
  1583.9 35.4 %all-reduce.3.cloned.1.call-done = f32[512,512]{0,1:T(8,128)} async-done(((f32[512,512]{0,1:T(8,128)}), f32[512,512]{0,1:T(8,128)}) %all-reduce.3.cloned.1.call-update) | async-done | bytes 1048592 | tf_op jit(solution)/shard_map/psum | solution.py:57
  1619.3 1.6 copy.9
  1620.9 1.4 fusion.10
  1622.4 11.7 cholesky.104
  1634.2 9.8 custom-call.31
  1644.7 11.7 cholesky.217
  1656.5 18.5 custom-call.32
  1675.7 11.7 cholesky.238
  1687.4 0.7 compare_reduce_fusion.1
  1688.1 9.8 custom-call.33
  1698.6 11.7 cholesky.255
  1710.3 0.6 compare_reduce_fusion
  1710.9 1.0 compare_reduce_fusion.2
  1714.7 10.9 while.1
  1714.8 0.6 fusion.67
  1715.3 2.0 bitcast_dynamic-update-slice_fusion.2
  1717.5 0.6 fusion.67
  1718.1 2.0 bitcast_dynamic-update-slice_fusion.2
  1720.2 0.6 fusion.67
  1720.8 2.0 bitcast_dynamic-update-slice_fusion.2
  1722.9 0.6 fusion.67
  1723.5 2.0 bitcast_dynamic-update-slice_fusion.2
  1725.5 40.1 %custom-call.34 = f32[4,128,128]{1,2,0:T(8,128)S(1)} custom-call(f32[4,128,128]{2,1,0:T(8,128)} %get-tuple-element.10), custom_call_target="InvertDiagBlocksLowerTriangular" | custom-call | tf_op jit(solution)/shard_map/jit(_solve_triangular)/triangular_solve | solution.py:38
  1765.7 1.1 fusion.21
  1767.1 0.4 fusion.33
  1768.0 0.4 fusion.31
  1768.4 0.6 convolution_subtract_fusion.2
  1769.1 0.4 fusion.30
  1769.5 17.1 fusion.2
  1786.6 3.2 copy-done
  1789.8 58.7 %fusion.45 = f32[2048,512]{1,0:T(8,128)} fusion(f32[4096,2048]{1,0:T(8,128)} %convolution_add_fusion, f32[4096,512]{1,0:T(8,128)S(1)} %fusion.2), kind=kOutput, calls=%fused_computation.87 | convolution fusion | flops 51539607552 | bytes 46137344 | tf_op jit(solution)/shard_map/dot_general | solution.py:16
  1848.7 45.2 %reduce-scatter.2.cloned.1.call-done = f32[512,512]{1,0:T(8,128)} async-done(((f32[2048,512]{1,0:T(8,128)}), f32[512,512]{1,0:T(8,128)}) %reduce-scatter.2.cloned.1.call-update) | async-done | bytes 1048592 | tf_op jit(solution)/shard_map/reduce_scatter | solution.py:59
  1893.8 1.3 multiply_reduce_fusion
  1895.2 39.7 %psum.15 = f32[512]{0:T(512)S(1)} all-reduce(f32[512]{0:T(512)S(1)} %multiply_reduce_fusion), channel_id=1, replica_groups=mesh['row'=4,'col'=8] {'row','col'}, use_global_device_ids=true, to_apply=%region_12.13 | all-reduce | flops 512 | bytes 4096 | tf_op jit(solution)/shard_map/psum | solution.py:62
  1934.8 2.3 broadcast_divide_fusion
  1937.2 62.5 %multiply_subtract_fusion = f32[4096,2048]{1,0:T(8,128)} fusion(f32[4096,2048]{1,0:T(8,128)} %convolution_add_fusion, f32[4096,512]{1,0:T(8,128)} %copy-done, f32[2048,512]{1,0:T(8,128)} %all-gather.13.cloned.1.call-done), kind=kOutput, calls=%fused_computation.2 | convolution fusion | flops 51556384768 | bytes 79691776 | tf_op jit(solution)/shard_map/dot_general | solution.py:26
  1999.7 59.6 %subtract_convert_fusion = bf16[4096,2048]{1,0:T(8,128)(2,1)} fusion(bf16[4096,2048]{1,0:T(8,128)(2,1)} %param.5, f32[4096,512]{1,0:T(8,128)} %copy-done, f32[2048,512]{1,0:T(8,128)S(1)} %copy-done.1, f32[512]{0:T(512)S(1)} %add_sqrt_fusion), kind=kOutput, calls=%fused_computation.3 | convolution fusion | flops 51574210560 | bytes 46139392 | tf_op jit(solution)/shard_map/dot_general | solution.py:26
  (42 shorter events, 4.1 us)
Async XLA Ops:
  7.2 39.6 %all-gather.9.cloned.1.call-start = ((), (), s32[]{:S(2)}) async-start(), calls=%async_computation.2 | async-start | bytes 5242880 | tf_op jit(solution)/shard_map/all_gather | solution.py:46
  7.9 165.5 %all-gather.7.cloned.1.call-start = ((), (), s32[]{:S(2)}) async-start(), calls=%async_computation.1 | async-start | bytes 9437184 | tf_op jit(solution)/shard_map/all_gather | solution.py:43
  8.6 201.0 %all-gather.11.cloned.1.call-start = ((), (), s32[]{:S(2)}) async-start(), calls=%async_computation.3 | async-start | bytes 5242880 | tf_op jit(solution)/shard_map/all_gather | solution.py:51
  9.4 1530.3 %all-gather.15.cloned.1.call-start = ((), (), s32[]{:S(2)}) async-start(), calls=%async_computation.7 | async-start | bytes 75497472 | tf_op jit(solution)/shard_map/all_gather | solution.py:55
  274.7 1344.6 %all-reduce.3.cloned.1.call-start = ((), (), s32[]{:S(2)}) async-start(), calls=%async_computation.4 | async-start | bytes 2097152 | tf_op jit(solution)/shard_map/psum | solution.py:57
  1582.9 310.9 %reduce-scatter.2.cloned.1.call-start = ((), (), s32[]{:S(2)}) async-start(), calls=%async_computation.5 | async-start | bytes 5242880 | tf_op jit(solution)/shard_map/reduce_scatter | solution.py:59
  1786.6 3.2 copy-start
  1848.6 88.6 %all-gather.13.cloned.1.call-start = ((), (), s32[]{:S(2)}) async-start(), calls=%async_computation.6 | async-start | bytes 5242880 | tf_op jit(solution)/shard_map/all_gather | solution.py:65
  1937.2 62.5 %copy-start.1 = (f32[2048,512]{1,0:T(8,128)S(1)}, f32[2048,512]{1,0:T(8,128)}, u32[]{:S(2)}) copy-start(f32[2048,512]{1,0:T(8,128)} %all-gather.13.cloned.1.call-done) | copy-start | bytes 12582916
Sparse Core Ops, SparseCore 0:
  9.5 37.1 all-gather.8
  48.9 124.4 all-gather.6
  174.9 32.6 all-gather.10
  274.8 1264.7 all-gather.14
  1583.0 36.2 all-reduce.2
  1848.7 45.0 reduce-scatter.1
  1895.4 34.7 all-gather.12
